TPU v7x, 32 devices: a whole 2x2x4 slice. The times are simulated.
32 devices in a mesh: groups: 1, ep: 16 (over z, y, x), role: 2 (over core).
Axes of the slice: x: 2, y: 2, z: 4, core: 2. Of those that a mesh axis runs over, the one named last changes fastest.
Arguments:
- residual: bfloat16 [192, 2880], P(('groups', 'ep', 'role')), may hold values from -1.796875 to 1.796875
- queries: bfloat16 [192, 2880], P(('groups', 'ep', 'role')), may hold values from -150 to 150
- key_new: bfloat16 [192, 320], P(('groups', 'ep', 'role')), may hold values from -6 to 6
- value_new: bfloat16 [192, 320], P(('groups', 'ep', 'role')), may hold values from -6 to 6
- key_cache: bfloat16 [192, 128, 320], P(('groups', 'ep', 'role')), may hold values from -6 to 6
- value_cache: bfloat16 [192, 128, 320], P(('groups', 'ep', 'role')), may hold values from -6 to 6
- lengths: int32 [192], P(('groups', 'ep', 'role')), may hold values from 1 to 512
- sink_logits: float32 [45], replicated, may hold values from -6 to 6
- norm_gain: float32 [2880], replicated, may hold values from 0.1 to 1.9
- route_ids: int32 [192, 4], P(('groups', 'ep')), may hold values from 0 to 7, all different within a row; in each aligned block of 12 rows (0 to 11, 12 to 23, ...) at most 6 rows name the same one
- route_logits: float32 [192, 4], P(('groups', 'ep')), may hold values from -1 to 1
- up_weight: bfloat16 [2880, 11520], P(None, ('ep', 'role')), may hold values from -0.109375 to 0.109375
- down_weight: bfloat16 [11520, 2880], P(('ep', 'role')), may hold values from -0.15625 to 0.15625
Outputs:
- layer_out: bfloat16 [192, 2880], P(('groups', 'ep', 'role'))
Inputs may be any that keep to these rules, and one draw needn't show every extreme that they name: `route_ids`: in each aligned block of 12 rows (the tokens of one index of ep) no expert is named more than 6 times, a bound that some block reaches.
All inputs are finite; a program needn't handle non-finite values.
Results may differ from a plain program's by a relative error of at most 0.0095.
Values may be sent and summed in bfloat16 or wider, within the bound.
A program may use at most 64 MiB of HBM per device.

v0:
```python
import jax
import jax.numpy as jnp
from jax import lax
from jax.sharding import PartitionSpec as P

HD = 64


def attention(queries, key_new, value_new, key_cache, value_cache, lengths, sink_logits):
    request_count = queries.shape[0]
    window = key_cache.shape[1]
    heads_kv = key_new.shape[1] // HD
    group_size = queries.shape[1] // (heads_kv * HD)
    query_heads = queries.reshape(request_count, heads_kv, group_size, HD)
    cached_keys = key_cache.reshape(request_count, window, heads_kv, HD)
    cached_values = value_cache.reshape(request_count, window, heads_kv, HD)
    fresh_key = key_new.reshape(request_count, heads_kv, HD)
    fresh_value = value_new.reshape(request_count, heads_kv, HD)
    score_scale = HD ** (-0.5)
    cached = (
        jnp.einsum("tkgd,tskd->tkgs", query_heads, cached_keys, preferred_element_type=jnp.float32)
        * score_scale
    )
    fresh_score = (
        jnp.einsum("tkgd,tkd->tkg", query_heads, fresh_key, preferred_element_type=jnp.float32)
        * score_scale
    )
    newest = lengths[:, None] - 1
    slot_index = jnp.arange(window, dtype=jnp.int32)[None, :]
    position = newest - jnp.mod(newest - slot_index, window)
    visible = (position >= 0) & (position >= lengths[:, None] - window + 1)
    cached = jnp.where(visible[:, None, None, :], cached, -1e30)
    sink_logit = sink_logits.reshape(1, heads_kv, group_size)
    highest = jnp.maximum(jnp.maximum(jnp.max(cached, -1), fresh_score), sink_logit)
    weights = jnp.exp(cached - highest[..., None])
    fresh_weight = jnp.exp(fresh_score - highest)
    denominator = jnp.sum(weights, -1) + fresh_weight + jnp.exp(sink_logit - highest)
    cache_probs = (weights / denominator[..., None]).astype(jnp.bfloat16)
    fresh_prob = (fresh_weight / denominator).astype(jnp.bfloat16)
    context = jnp.einsum(
        "tkgs,tskd->tkgd", cache_probs, cached_values, preferred_element_type=jnp.float32
    )
    context = (
        context
        + fresh_prob.astype(jnp.float32)[..., None] * fresh_value.astype(jnp.float32)[:, :, None, :]
    )
    return context.reshape(request_count, -1)


def local(
    residual,
    queries,
    key_new,
    value_new,
    key_cache,
    value_cache,
    lengths,
    sink_logits,
    norm_gain,
    route_ids,
    route_logits,
    up_weight,
    down_weight,
):
    context = attention(queries, key_new, value_new, key_cache, value_cache, lengths, sink_logits)
    hidden_state = residual.astype(jnp.float32) + context
    normed = (
        hidden_state
        * lax.rsqrt(jnp.mean(hidden_state * hidden_state, -1, keepdims=True) + 1e-05)
        * norm_gain
    ).astype(jnp.bfloat16)
    gate_weights = jax.nn.softmax(route_logits, axis=-1)
    pair_count, pick_count = route_ids.shape
    rank_count = lax.axis_size("ep")
    experts = rank_count // 2
    capacity = min(pair_count, max(2, (pair_count * pick_count + experts - 1) // experts))
    width = residual.shape[1]
    tok_rows = lax.all_gather(normed, "role", axis=0, tiled=True)
    onehot = (route_ids[..., None] == jnp.arange(experts, dtype=jnp.int32)).astype(jnp.int32)
    flat_hot = onehot.reshape(-1, experts)
    earlier = jnp.cumsum(flat_hot, axis=0) - flat_hot
    slot_number = jnp.sum(earlier * flat_hot, -1).reshape(pair_count, pick_count)
    slot_hot = (slot_number[..., None] == jnp.arange(capacity, dtype=jnp.int32)).astype(jnp.float32)
    selector = (onehot.astype(jnp.float32)[..., :, None] * slot_hot[..., None, :]).reshape(
        pair_count, pick_count, experts * capacity
    )
    dispatch = jnp.sum(selector, 1).astype(jnp.bfloat16)
    mixing = jnp.sum(selector * gate_weights[..., None], 1)
    packed = jnp.einsum("te,td->ed", dispatch, tok_rows, preferred_element_type=jnp.float32).astype(
        jnp.bfloat16
    )
    outgoing = jnp.repeat(packed.reshape(experts, capacity, width), 2, axis=0)
    received = lax.all_to_all(outgoing, "ep", split_axis=0, concat_axis=0, tiled=True)
    gathered = received.reshape(-1, width)
    activation = jax.nn.silu(
        jnp.dot(gathered, up_weight, preferred_element_type=jnp.float32)
    ).astype(jnp.bfloat16)
    partial_value = jnp.dot(activation, down_weight, preferred_element_type=jnp.float32).astype(
        jnp.bfloat16
    )
    returned_rows = lax.all_to_all(
        partial_value.reshape(received.shape[0], received.shape[1], width),
        "ep",
        split_axis=0,
        concat_axis=0,
        tiled=True,
    )
    pair_sum = jnp.sum(
        returned_rows.astype(jnp.float32).reshape(experts, 2, capacity, width), 1
    ).reshape(experts * capacity, width)
    mixed = jnp.dot(mixing, pair_sum, precision=lax.Precision.HIGHEST)
    expert_out = lax.psum_scatter(
        mixed.astype(jnp.bfloat16), "role", scatter_dimension=0, tiled=True
    ).astype(jnp.float32)
    return (hidden_state + expert_out).astype(jnp.bfloat16)


def solution(mesh):
    placed = (
        P(("groups", "ep", "role"), None),
        P(("groups", "ep", "role"), None),
        P(("groups", "ep", "role"), None),
        P(("groups", "ep", "role"), None),
        P(("groups", "ep", "role"), None, None),
        P(("groups", "ep", "role"), None, None),
        P(("groups", "ep", "role")),
        P(),
        P(),
        P(("groups", "ep"), None),
        P(("groups", "ep"), None),
        P(None, ("ep", "role")),
        P(("ep", "role"), None),
    )
    return jax.shard_map(
        local,
        mesh=mesh,
        in_specs=placed,
        out_specs=P(("groups", "ep", "role"), None),
        check_vma=False,
    )
```

profile of v0, /device:TPU:25, one launch (start us, length us, event | category | flops | bytes accessed | tf_op | source)
XLA Modules:
  0.0 104.3 jit_solution(4723980325526437629)
XLA Ops:
  6.5 0.0 copy-start
  6.5 0.0 all-reduce.3.cloned.1.call-start
  6.5 0.9 copy.24
  7.5 0.7 convert_convert_fusion
  8.2 0.1 eq.50
  8.2 0.1 fusion.13
  8.3 0.1 reduce_window_sum.11
  8.4 0.2 select_reduce_fusion
  8.6 0.1 eq.54
  8.7 0.1 copy.25
  8.8 0.7 reduce_max.19
  9.5 0.7 fusion.22
  10.2 0.7 fusion.21
  10.9 0.6 multiply_reduce_fusion
  11.5 0.2 copy.26
  11.7 0.1 convert_element_type.85
  11.7 0.9 reshape.133
  12.7 0.7 broadcast_add_fusion.1
  13.3 0.8 reshape.144
  14.1 0.8 reshape.153
  14.9 0.7 max.15
  15.6 0.1 compare_and_fusion
  15.7 0.2 fusion.27
  15.8 1.4 %fusion.24 = (f32[6,5,9]{2,1,0:T(8,128)S(1)}, f32[6,5,9,128]{3,2,1,0:T(8,128)S(1)}) fusion(bf16[6,5,9,64]{3,2,1,0:T(8,128)(2,1)S(1)} %reshape.133, bf16[6,128,5,64]{1,3,2,0:T(8,128)(2,1)} %bitcast.40, pred[6,128]{1,0:T(8,128)(4,1)S(1)} %compare_and_fusion), kind=kOutput, calls=%fused_computation.55 | convolution fusion | flops 4527090 | bytes 666168 | tf_op jit(solution)/shard_map/tkgd,tskd->tkgs/dot_general | solution.py:21
  17.2 0.3 fusion.3
  17.5 1.5 %convolution_add_fusion = f32[6,5,9,64]{3,2,1,0:T(8,128)S(1)} fusion(bf16[6,128,5,64]{1,3,2,0:T(8,128)(2,1)} %bitcast.41, f32[6,5,9,128]{3,2,1,0:T(8,128)S(1)} %get-tuple-element.12, f32[6,5,64]{2,1,0:T(8,128)S(1)} %reshape.144, f32[6,5,9]{2,1,0:T(8,128)S(1)} %get-tuple-element.7, f32[6,5,9]{2,1,0:T(8,128)S(1)} %get-tuple-element.8, f32[6,5,9]{2,1,0:T(8,128)S(1)} %fusion.11), kind=kOutput, calls=%fused_computation.5 | convolution fusion | flops 4561920 | bytes 709800 | tf_op jit(solution)/shard_map/tkgs,tskd->tkgd/dot_general | solution.py:40
  19.0 0.1 reshape.137
  19.1 0.1 multiply_reduce_fusion.1
  19.3 0.1 fusion.8
  19.4 2.2 %all-gather = bf16[2,6,2880]{2,1,0:T(8,128)(2,1)S(1)} all-gather(bf16[1,6,2880]{2,1,0:T(8,128)(2,1)S(1)} %fusion.8), channel_id=1, replica_groups=mesh['groups'=1,'ep'=16,'role'=2] {'role'}, dimensions={0}, use_global_device_ids=true | all-gather | bytes 103680 | tf_op jit(solution)/shard_map/all_gather | solution.py:78
  21.6 0.1 reshape.148
  21.6 0.3 convolution_convert_fusion.1
  21.9 0.1 reshape.138
  22.0 0.1 broadcast_in_dim.16
  22.1 24.6 %all_to_all.10 = bf16[16,6,2880]{2,1,0:T(8,128)(2,1)S(1)} all-to-all(bf16[16,6,2880]{2,1,0:T(8,128)(2,1)S(1)} %bitcast.39), channel_id=1, replica_groups=mesh['groups'=1,'ep'=16,'role'=2] {'ep'}, dimensions={0} | all-to-all | bytes 1105920 | tf_op jit(solution)/shard_map/all_to_all | solution.py:93
  46.6 0.3 reshape.140
  47.0 4.0 %convolution_convert_fusion = bf16[96,2880]{1,0:T(8,128)(2,1)} fusion(bf16[360,2880]{1,0:T(8,128)(2,1)S(1)} %copy-done, bf16[96,2880]{1,0:T(8,128)(2,1)S(1)} %reshape.140, bf16[2880,360]{0,1:T(8,128)(2,1)} %param.24), kind=kOutput, calls=%fused_computation | convolution fusion | flops 398580480 | bytes 5253120 | tf_op jit(solution)/shard_map/dot_general | solution.py:98
  51.0 1.3 %reshape.141 = bf16[16,6,2880]{2,1,0:T(8,128)(2,1)S(1)} reshape(bf16[96,2880]{1,0:T(8,128)(2,1)} %convolution_convert_fusion) | data formatting | bytes 1105920 | tf_op jit(solution)/shard_map/reshape | solution.py:102
  52.3 0.0 copy-start.5
  52.3 0.0 copy-start.2
  52.3 23.4 %all_to_all.11 = bf16[16,6,2880]{2,1,0:T(8,128)(2,1)S(1)} all-to-all(bf16[16,6,2880]{2,1,0:T(8,128)(2,1)S(1)} %reshape.141), channel_id=1, replica_groups=mesh['groups'=1,'ep'=16,'role'=2] {'ep'}, dimensions={0} | all-to-all | bytes 1105920 | tf_op jit(solution)/shard_map/all_to_all | solution.py:101
  75.7 0.2 convert_reduce_fusion
  75.9 1.1 %fusion = bf16[12,2880]{1,0:T(8,128)(2,1)} fusion(f32[12,8,6]{0,1,2:T(8,128)S(1)} %copy-done.3, f32[8,6,2880]{2,1,0:T(8,128)S(1)} %convert_reduce_fusion), kind=kOutput, calls=%fused_computation.3 | convolution fusion | flops 19941120 | bytes 624384 | tf_op jit(solution)/shard_map/dot_general | solution.py:111
  77.0 0.0 all-reduce.3.cloned.1.call-update
  77.1 0.6 dynamic-slice
  78.3 17.6 %all-reduce.3.cloned.1.call-done = bf16[12,2880]{1,0:T(8,128)(2,1)} async-done(((bf16[12,2880]{1,0:T(8,128)(2,1)}), bf16[12,2880]{1,0:T(8,128)(2,1)}) %all-reduce.3.cloned.1.call-update) | async-done | bytes 69136
  95.9 0.0 copy-done.2
  95.9 1.5 %add_convert_fusion = bf16[6,2880]{1,0:T(8,128)(2,1)} fusion(bf16[12,2880]{1,0:T(8,128)(2,1)} %all-reduce.3.cloned.1.call-done, u32[]{:T(128)S(6)} %multiply.7, f32[6,2880]{1,0:T(8,128)S(1)} %reshape.137, bf16[6,2880]{1,0:T(8,128)(2,1)S(1)} %copy-done.2), kind=kLoop, calls=%fused_computation.18 | loop fusion | flops 86400 | bytes 172804 | tf_op jit(solution)/shard_map/convert_element_type | solution.py:115
  (12 shorter events, 0.1 us)
Async XLA Ops:
  6.5 40.4 %copy-start = (bf16[360,2880]{1,0:T(8,128)(2,1)S(1)}, bf16[360,2880]{1,0:T(8,128)(2,1)}, u32[]{:S(2)}) copy-start(bf16[360,2880]{1,0:T(8,128)(2,1)} %param.25) | copy-start | bytes 6220804
  6.5 12.6 %copy-start.1 = (bf16[6,2880]{1,0:T(8,128)(2,1)S(1)}, bf16[6,2880]{1,0:T(8,128)(2,1)}, u32[]{:S(2)}) copy-start(bf16[6,2880]{1,0:T(8,128)(2,1)} %param.13) | copy-start | bytes 103684
  6.5 12.7 %copy-start.4 = (f32[2880]{0:T(1024)S(1)}, f32[2880]{0:T(1024)}, u32[]{:S(2)}) copy-start(f32[2880]{0:T(1024)} %param.21) | copy-start | bytes 34564
  6.5 89.4 %all-reduce.3.cloned.1.call-start = ((), (), s32[]{:S(2)}) async-start(), calls=%async_computation.2 | async-start | bytes 188416
  51.0 24.9 %copy-start.3 = (f32[12,8,6]{0,1,2:T(8,128)S(1)}, f32[12,8,6]{0,1,2:T(8,128)}, u32[]{:S(2)}) copy-start(f32[12,8,6]{0,1,2:T(8,128)} %get-tuple-element.6) | copy-start | bytes 6916
  52.3 24.8 %copy-start.5 = (u32[32]{0:T(128)S(1)}, u32[32]{0:T(128)}, u32[]{:S(2)}) copy-start(u32[32]{0:T(128)} %constant.59) | copy-start | bytes 388
  52.3 43.6 %copy-start.2 = (bf16[6,2880]{1,0:T(8,128)(2,1)S(1)}, bf16[6,2880]{1,0:T(8,128)(2,1)}, u32[]{:S(2)}) copy-start(bf16[6,2880]{1,0:T(8,128)(2,1)} %param.13) | copy-start | bytes 103684
Sparse Core Ops, SparseCore 0:
  77.2 18.7 all-reduce.2
where the time goes:
time: 106 us; the launch traced here: 104 us
  blocking collectives  50.2 us (47%)
  waiting for transfers between devices  17.7 us (17%)
  between operations  14.2 us (13%)
  matrix products  8.4 us (8%)
  local copies, waits for them, and re-layouts  7.15 us (7%)
  other arithmetic  6.75 us (6%)
    all_to_all x1, blocking collectives, local(): lax.all_to_all(outgoing, 'ep', split_axis=0, concat_axis=0, tiled=True)  24.6 us
    all_to_all x1, blocking collectives, local(): lax.all_to_all(partial_value.reshape(received.shape[0], received.shape[1]...  23.4 us
    unnamed x2, waiting for transfers between devices  17.7 us
    dot_general x1, matrix products, local(): jnp.dot(activation, down_weight, preferred_element_type=jnp.float32)  4.04 us
    all_gather x1, blocking collectives, local(): tok_rows = lax.all_gather(normed, 'role', axis=0, tiled=True)  2.2 us
  transfers between devices with their start and end apart: 1, of which 1 were waited for; matrix products, arithmetic and copies ran while one was open for 1% of the time, Pallas kernels for 0%

commit v1 on v0

v1 whole, which is shorter than its diff:
```python
import functools

import jax
import jax.numpy as jnp
from jax import lax
from jax.experimental import pallas as pl
from jax.experimental.pallas import tpu as pltpu
from jax.sharding import PartitionSpec as P

HD = 64
LANES = 128
SLOTS = 8
MESH = pl.DeviceIdType.MESH
BF16 = jnp.bfloat16
F32 = jnp.float32


def iota(shape, dim):
    return lax.broadcasted_iota(jnp.int32, shape, dim)


def spread_queries(q_ref, wide_ref, group_size):
    rows, width = q_ref.shape
    heads = width // HD
    wide_ref[...] = jnp.zeros_like(wide_ref)
    kv_width = wide_ref.shape[2]
    for head in range(heads):
        tile, half = head // 2, head % 2
        size = min(LANES, width - tile * LANES)
        block = q_ref[:, tile * LANES : tile * LANES + size].astype(F32)
        if size < LANES:
            block = jnp.concatenate([block, jnp.zeros((rows, LANES - size), F32)], axis=1)
        kv = head // group_size
        if half != kv % 2:
            block = pltpu.roll(block, HD, 1)
        lane = iota(block.shape, 1)
        block = jnp.where((lane // HD) == (kv % 2), block, 0.0)
        start = (kv // 2) * LANES
        stop = min(start + LANES, kv_width)
        wide_ref[:, head, start:stop] = block[:, : stop - start]


def attend(wide_ref, kn_ref, vn_ref, k_ref, v_ref, len_ref, sink_ref, ctx_ref, group_size):
    requests, head_rows, kv_width = wide_ref.shape
    window = k_ref.shape[1]
    heads = sink_ref.shape[1]
    scale = HD ** (-0.5)
    eye = iota((head_rows, heads), 0) == iota((head_rows, heads), 1)
    sink = jnp.sum(jnp.where(eye, sink_ref[...], 0.0), axis=1, keepdims=True)
    own = (iota((head_rows, kv_width), 0) // group_size) == (iota((head_rows, kv_width), 1) // HD)
    slot = iota((1, window), 1)
    for t in range(requests):
        length = len_ref[t]
        newest = length - 1
        behind = lax.rem(newest, window) - slot
        behind = jnp.where(behind < 0, behind + window, behind)
        position = newest - behind
        visible = (position >= 0) & (position >= length - window + 1)
        q = wide_ref[t]
        scores = (
            lax.dot_general(
                q.astype(BF16), k_ref[t], (((1,), (1,)), ((), ())), preferred_element_type=F32
            )
            * scale
        )
        scores = jnp.where(visible, scores, -1e30)
        fresh = (
            jnp.sum(q * kn_ref[t : t + 1, :].astype(F32), axis=1, keepdims=True) * scale
        )
        highest = jnp.maximum(
            jnp.maximum(jnp.max(scores, axis=1, keepdims=True), fresh), sink
        )
        weights = jnp.exp(scores - highest)
        fresh_weight = jnp.exp(fresh - highest)
        total = jnp.sum(weights, axis=1, keepdims=True) + fresh_weight + jnp.exp(sink - highest)
        probs = (weights / total).astype(BF16)
        fresh_prob = (fresh_weight / total).astype(BF16).astype(F32)
        context = jnp.dot(probs, v_ref[t], preferred_element_type=F32)
        context = context + fresh_prob * vn_ref[t : t + 1, :].astype(F32)
        context = jnp.where(own, context, 0.0)
        folded = jnp.zeros((head_rows, LANES), F32)
        for start in range(0, kv_width, LANES):
            part = context[:, start : min(start + LANES, kv_width)]
            if part.shape[1] < LANES:
                part = jnp.concatenate(
                    [part, jnp.zeros((head_rows, LANES - part.shape[1]), F32)], axis=1
                )
            folded = folded + part
        ctx_ref[t] = folded + pltpu.roll(folded, HD, 1)


def kernel(
    n,
    capacity,
    half,
    q_ref,
    res_ref,
    kn_ref,
    vn_ref,
    len_ref,
    sink_ref,
    gain_ref,
    ids_ref,
    logit_ref,
    k_hbm,
    v_hbm,
    up_hbm,
    down_hbm,
    out_ref,
    k_ref,
    v_ref,
    up_ref,
    down_ref,
    wide_ref,
    ctx_ref,
    hid_ref,
    norm_ref,
    rows_ref,
    ids_pad,
    logit_pad,
    packed_ref,
    recv_ref,
    act_ref,
    down_half,
    down_peer,
    sent_ref,
    back_ref,
    mix_ref,
    mix_peer,
    load_sem,
    one_send,
    one_recv,
    go_send,
    go_recv,
    fwd_send,
    fwd_recv,
    ret_send,
    ret_recv,
):
    me = lax.axis_index("ep")
    core = lax.axis_index("role")
    group = lax.axis_index("groups")
    peer = (group, me, 1 - core)
    rows, width = res_ref.shape
    heads = width // HD
    experts = n // 2
    group_size = heads // (kn_ref.shape[1] // HD)
    depth = down_ref.shape[0]

    loads = [
        pltpu.make_async_copy(src, dst, load_sem.at[i])
        for i, (src, dst) in enumerate(
            ((k_hbm, k_ref), (v_hbm, v_ref), (down_hbm, down_ref), (up_hbm, up_ref))
        )
    ]
    for load in loads:
        load.start()

    recv_ref[...] = jnp.zeros_like(recv_ref)
    back_ref[...] = jnp.zeros_like(back_ref)

    barrier = pltpu.get_barrier_semaphore()
    pl.semaphore_signal(barrier, inc=1, device_id=peer, device_id_type=MESH)

    @pl.loop(1, n)
    def _(step):
        other = lax.rem(me + step, n)
        pl.semaphore_signal(barrier, inc=1, device_id=(group, other, core), device_id_type=MESH)

    token_rows = 2 * SLOTS
    ids_pad[...] = jnp.full(ids_pad.shape, -1, jnp.int32)
    logit_pad[...] = jnp.zeros(logit_pad.shape, F32)
    for side in range(2):
        ids_pad[side * SLOTS : side * SLOTS + rows, :] = ids_ref[side * rows : (side + 1) * rows, :]
        logit_pad[side * SLOTS : side * SLOTS + rows, :] = logit_ref[
            side * rows : (side + 1) * rows, :
        ]
    ids = ids_pad[...]
    logits = logit_pad[...]
    gates = jnp.exp(logits - jnp.max(logits, axis=1, keepdims=True))
    gates = gates / jnp.sum(gates, axis=1, keepdims=True)
    earlier = (iota((token_rows, token_rows), 1) < iota((token_rows, token_rows), 0)).astype(F32)

    def tables(columns, per_expert):
        shape = (token_rows, columns)
        expert = iota(shape, 1) // per_expert
        slot = lax.rem(iota(shape, 1), SLOTS)
        hot = jnp.zeros(shape, F32)
        gate = jnp.zeros(shape, F32)
        for pick in range(ids.shape[1]):
            named = ids[:, pick : pick + 1] == expert
            hot = hot + jnp.where(named, 1.0, 0.0)
            gate = gate + jnp.where(named, gates[:, pick : pick + 1], 0.0)
        place = jnp.dot(earlier.astype(BF16), hot.astype(BF16), preferred_element_type=F32)
        chosen = jnp.where(place == slot.astype(F32), hot, 0.0)
        return chosen, gate * chosen

    spread_queries(q_ref, wide_ref, group_size)
    loads[0].wait()
    loads[1].wait()
    attend(wide_ref, kn_ref, vn_ref, k_ref, v_ref, len_ref, sink_ref, ctx_ref, group_size)
    hid_ref[...] = jnp.zeros_like(hid_ref)
    for tile in range((heads + 1) // 2):
        first = ctx_ref[:, 2 * tile, :]
        if 2 * tile + 1 < heads:
            second = ctx_ref[:, 2 * tile + 1, :]
        else:
            second = jnp.zeros_like(first)
        size = min(LANES, width - tile * LANES)
        both = jnp.where(iota(first.shape, 1) < HD, first, second)[:, :size]
        columns = slice(tile * LANES, tile * LANES + size)
        hid_ref[0:rows, columns] = both + res_ref[:, columns].astype(F32)
    hidden = hid_ref[...]
    inverse = lax.rsqrt(jnp.sum(hidden * hidden, axis=1, keepdims=True) / width + 1e-05)
    norm_ref[0] = (hidden[:, :half] * inverse * gain_ref[:, :half]).astype(BF16)
    norm_ref[1] = jnp.zeros(norm_ref.shape[1:], BF16)
    norm_ref[1, :, : width - half] = (
        hidden[:, half:width] * inverse * gain_ref[:, half:]
    ).astype(BF16)

    pl.semaphore_wait(barrier, n)

    def to_peer(src, dst, number):
        return pltpu.make_async_remote_copy(
            src_ref=src,
            dst_ref=dst,
            send_sem=one_send.at[number],
            recv_sem=one_recv.at[number],
            device_id=peer,
            device_id_type=MESH,
        )

    swap_rows = to_peer(norm_ref.at[1 - core], rows_ref.at[core], 0)
    swap_rows.start()
    rows_ref[core] = norm_ref[core]

    loads[2].wait()
    down_half[0] = down_ref[:, :half]
    down_half[1] = jnp.zeros(down_half.shape[1:], BF16)
    down_half[1, :, : width - half] = down_ref[:, half:]

    send_table, _ = tables(max(experts * SLOTS, LANES), SLOTS)
    send_table = send_table.T[: experts * SLOTS].astype(BF16)
    swap_rows.wait()
    token_block = rows_ref[...].astype(F32).reshape(token_rows, half).astype(BF16)
    packed = jnp.dot(send_table, token_block, preferred_element_type=F32)
    packed_ref[...] = packed.reshape(experts, SLOTS, half).astype(BF16)

    used = pl.ds(0, capacity)

    def go(step):
        other = lax.rem(me + step, n)
        return pltpu.make_async_remote_copy(
            src_ref=packed_ref.at[other // 2, used],
            dst_ref=recv_ref.at[core, me, used],
            send_sem=go_send.at[other],
            recv_sem=go_recv.at[me],
            device_id=(group, other, core),
            device_id_type=MESH,
        )

    def come(step, buffer, send_sem, recv_sem):
        source = lax.rem(me + n - step, n)
        return source, pltpu.make_async_remote_copy(
            src_ref=buffer,
            dst_ref=buffer,
            send_sem=send_sem.at[source],
            recv_sem=recv_sem.at[source],
            device_id=peer,
            device_id_type=MESH,
        )

    @pl.loop(1, n)
    def _(step):
        go(step).start()

    swap_down = to_peer(down_half.at[1 - core], down_peer, 1)
    swap_down.start()

    def forward(src, source):
        return pltpu.make_async_remote_copy(
            src_ref=src,
            dst_ref=recv_ref.at[core, source, used],
            send_sem=fwd_send.at[source],
            recv_sem=fwd_recv.at[source],
            device_id=peer,
            device_id_type=MESH,
        )

    recv_ref[core, me] = packed_ref[me // 2]
    forward(packed_ref.at[me // 2, used], me).start()

    @pl.loop(1, n)
    def _(step):
        source = lax.rem(me + n - step, n)
        block = recv_ref.at[core, source, used]
        come(step, block, go_send, go_recv)[1].wait_recv()
        forward(block, source).start()

    @pl.loop(0, n)
    def _(source):
        block = recv_ref.at[1 - core, source, used]
        pltpu.make_async_remote_copy(
            src_ref=block,
            dst_ref=block,
            send_sem=fwd_send.at[source],
            recv_sem=fwd_recv.at[source],
            device_id=peer,
            device_id_type=MESH,
        ).wait_recv()

    loads[3].wait()
    chunk = min(n, 16)
    chunk_rows = chunk * SLOTS

    @pl.loop(0, n // chunk)
    def _(part):
        blocks = pl.ds(part * chunk, chunk)
        low = recv_ref[0, blocks].astype(F32).reshape(chunk_rows, half).astype(BF16)
        high = recv_ref[1, blocks].astype(F32).reshape(chunk_rows, half).astype(BF16)
        value = jnp.dot(low, up_ref[:half, :], preferred_element_type=F32) + jnp.dot(
            high[:, : width - half], up_ref[half:, :], preferred_element_type=F32
        )
        value = value / (1.0 + jnp.exp(-value))
        act_ref[core, pl.ds(pl.multiple_of(part * chunk_rows, chunk_rows), chunk_rows), :] = (
            value.astype(BF16)
        )

    swap_act = to_peer(act_ref.at[core], act_ref.at[core], 2)
    swap_act.start()
    swap_down.wait()
    swap_act.wait()

    @pl.loop(0, n // chunk)
    def _(part):
        blocks = pl.ds(part * chunk, chunk)
        place = pl.ds(pl.multiple_of(part * chunk_rows, chunk_rows), chunk_rows)
        value = jnp.dot(
            act_ref[core, place, :], down_half[core], preferred_element_type=F32
        ) + jnp.dot(act_ref[1 - core, place, :], down_peer[...], preferred_element_type=F32)
        sent_ref[blocks] = value.reshape(chunk, SLOTS, half).astype(BF16)

    def give_back(step):
        other = lax.rem(me + step, n)
        return pltpu.make_async_remote_copy(
            src_ref=sent_ref.at[other, used],
            dst_ref=back_ref.at[me, used],
            send_sem=ret_send.at[other],
            recv_sem=ret_recv.at[me],
            device_id=(group, other, core),
            device_id_type=MESH,
        )

    @pl.loop(1, n)
    def _(step):
        give_back(step).start()

    back_ref[me] = sent_ref[me]
    _, mixing = tables(n * SLOTS, 2 * SLOTS)
    coarse = mixing.astype(BF16)
    fine = (mixing - coarse.astype(F32)).astype(BF16)

    @pl.loop(1, n)
    def _(step):
        go(step).wait_send()

    @pl.loop(0, n)
    def _(source):
        forward(recv_ref.at[core, source, used], source).wait_send()

    @pl.loop(1, n)
    def _(step):
        source = lax.rem(me + n - step, n)
        come(step, back_ref.at[source, used], ret_send, ret_recv)[1].wait_recv()

    returned = back_ref[...].astype(F32).reshape(n * SLOTS, half).astype(BF16)
    mixed = jnp.dot(coarse, returned, preferred_element_type=F32) + jnp.dot(
        fine, returned, preferred_element_type=F32
    )
    mix_ref[...] = mixed.reshape(2, SLOTS, half).astype(BF16)
    swap_mix = to_peer(mix_ref.at[1 - core], mix_peer, 3)
    swap_mix.start()
    mine = jnp.where(core == 0, mixed[:SLOTS], mixed[SLOTS:])

    @pl.loop(1, n)
    def _(step):
        give_back(step).wait_send()

    swap_mix.wait()
    theirs = mix_peer[...].astype(F32)
    low = jnp.where(core == 0, mine, theirs)
    high = jnp.where(core == 0, theirs, mine)
    out_ref[:, :half] = (hid_ref[:, :half] + low)[:rows].astype(BF16)
    out_ref[:, half:] = (hid_ref[:, half:width] + high[:, : width - half])[:rows].astype(BF16)


def local(
    residual,
    queries,
    key_new,
    value_new,
    key_cache,
    value_cache,
    lengths,
    sink_logits,
    norm_gain,
    route_ids,
    route_logits,
    up_weight,
    down_weight,
):
    n = lax.axis_size("ep")
    experts = n // 2
    pair_count, pick_count = route_ids.shape
    capacity = min(pair_count, max(2, (pair_count * pick_count + experts - 1) // experts))
    rows, width = residual.shape
    half = -(-width // (4 * LANES)) * 2 * LANES
    heads = width // HD
    head_rows = -(-heads // 8) * 8
    depth = up_weight.shape[1]
    vmem = pl.BlockSpec(memory_space=pltpu.VMEM)
    smem = pl.BlockSpec(memory_space=pltpu.SMEM)
    anywhere = pl.BlockSpec(memory_space=pl.ANY)
    dma = pltpu.SemaphoreType.DMA
    return pl.pallas_call(
        functools.partial(kernel, n, capacity, half),
        out_shape=jax.ShapeDtypeStruct((rows, width), BF16),
        in_specs=[vmem] * 4 + [smem] + [vmem] * 4 + [anywhere] * 4,
        out_specs=vmem,
        scratch_shapes=[
            pltpu.VMEM(key_cache.shape, BF16),
            pltpu.VMEM(value_cache.shape, BF16),
            pltpu.VMEM(up_weight.shape, BF16),
            pltpu.VMEM(down_weight.shape, BF16),
            pltpu.VMEM((rows, head_rows, key_new.shape[1]), F32),
            pltpu.VMEM((rows, head_rows, LANES), F32),
            pltpu.VMEM((SLOTS, 2 * half), F32),
            pltpu.VMEM((2, SLOTS, half), BF16),
            pltpu.VMEM((2, SLOTS, half), BF16),
            pltpu.VMEM((2 * SLOTS, pick_count), jnp.int32),
            pltpu.VMEM((2 * SLOTS, pick_count), F32),
            pltpu.VMEM((experts, SLOTS, half), BF16),
            pltpu.VMEM((2, n, SLOTS, half), BF16),
            pltpu.VMEM((2, n * SLOTS, depth), BF16),
            pltpu.VMEM((2, depth, half), BF16),
            pltpu.VMEM((depth, half), BF16),
            pltpu.VMEM((n, SLOTS, half), BF16),
            pltpu.VMEM((n, SLOTS, half), BF16),
            pltpu.VMEM((2, SLOTS, half), BF16),
            pltpu.VMEM((SLOTS, half), BF16),
            dma((4,)),
            dma((4,)),
            dma((4,)),
            dma((n,)),
            dma((n,)),
            dma((n,)),
            dma((n,)),
            dma((n,)),
            dma((n,)),
        ],
        compiler_params=pltpu.CompilerParams(
            collective_id=0, has_side_effects=True, vmem_limit_bytes=60 * 1024 * 1024
        ),
    )(
        queries,
        residual,
        key_new,
        value_new,
        lengths,
        sink_logits.reshape(1, -1),
        norm_gain.reshape(1, -1),
        route_ids,
        route_logits,
        key_cache,
        value_cache,
        up_weight,
        down_weight,
    )


def solution(mesh):
    placed = (
        P(("groups", "ep", "role"), None),
        P(("groups", "ep", "role"), None),
        P(("groups", "ep", "role"), None),
        P(("groups", "ep", "role"), None),
        P(("groups", "ep", "role"), None, None),
        P(("groups", "ep", "role"), None, None),
        P(("groups", "ep", "role")),
        P(),
        P(),
        P(("groups", "ep"), None),
        P(("groups", "ep"), None),
        P(None, ("ep", "role")),
        P(("ep", "role"), None),
    )
    return jax.shard_map(
        local,
        mesh=mesh,
        in_specs=placed,
        out_specs=P(("groups", "ep", "role"), None),
        check_vma=False,
    )
```

time: 106 us -> 43.1 us (0.41); the launches traced: 104 us -> 42.7 us
  blocking collectives: 50.2 us -> 0 us
  Pallas kernels: 0 us -> 30.4 us
  waiting for transfers between devices: 17.7 us -> 0 us
  between operations: 14.2 us -> 0.01 us
  matrix products: 8.4 us -> 0 us
  other arithmetic: 6.75 us -> 0 us
  local copies, waits for them, and re-layouts: 7.15 us -> 12.4 us
    all_to_all x2 -> x0, blocking collectives: 48 us -> none  [the longest x1 24.6 us: local(): lax.all_to_all(outgoing, 'ep', split_axis=0, concat_axis=0, tiled=True)]
    pallas_call x0 -> x1, Pallas kernels: none -> 30.4 us  [local(): pl.pallas_call(functools.partial(kernel, n, capacity, half), out_shape=ja...]
    unnamed x2 -> x0, waiting for transfers between devices: 17.7 us -> none
    unnamed x15 -> x8, local copies, waits for them, and re-layouts: 1.59 us -> 11 us
    dot_general x6 -> x0, matrix products: 8.4 us -> none  [the longest x1 4.04 us: local(): jnp.dot(activation, down_weight, preferred_element_type=jnp.float32)]
    convert_element_type x5 -> x0, other arithmetic: 2.34 us -> none  [the longest x1 1.54 us: local(): return (hidden_state + expert_out).astype(jnp.bfloat16)]
    reshape x6 -> x1, local copies, waits for them, and re-layouts: 3.51 us -> 1.31 us  [local(): norm_gain.reshape(1, -1)]
    all_gather x1 -> x0, blocking collectives: 2.2 us -> none  [local(): tok_rows = lax.all_gather(normed, 'role', axis=0, tiled=True)]
  transfers between devices with their start and end apart: 1 -> 0, of which waited for: 1 -> 0; matrix products, arithmetic and copies ran while one was open for 1% -> 0% of each run, Pallas kernels for 0% -> 0%
where the time goes in v1:
time: 43.1 us; the launch traced here: 42.7 us
  Pallas kernels  30.4 us (71%)
  local copies, waits for them, and re-layouts  12.4 us (29%)
    pallas_call x1, Pallas kernels, local(): pl.pallas_call(functools.partial(kernel, n, capacity, half), out_shape=ja...  30.4 us
    unnamed x8, local copies, waits for them, and re-layouts  11 us
    reshape x1, local copies, waits for them, and re-layouts, local(): norm_gain.reshape(1, -1)  1.31 us

profile of v1, /device:TPU:25, one launch (start us, length us, event | category | flops | bytes accessed | tf_op | source)
XLA Modules:
  0.0 42.7 jit_solution(10499822404689680409)
XLA Ops:
  0.0 0.0 copy-start
  0.0 1.5 %copy.14.ids_ref = s32[12,4]{1,0:T(8,128)} copy(s32[12,4]{0,1:T(4,128)} %param.22) | data formatting | bytes 384 | tf_op args[9]
  1.5 1.4 %copy.15.logit_ref = f32[12,4]{1,0:T(8,128)} copy(f32[12,4]{0,1:T(4,128)} %param.23) | data formatting | bytes 384 | tf_op args[10]
  2.9 1.3 %reshape.7.gain_ref = f32[1,2880]{1,0:T(1,128)} reshape(f32[2880]{0:T(1024)} %param.21) | data formatting | bytes 23040 | tf_op jit(solution)/shard_map/reshape | solution.py:471
  4.2 2.1 %copy.16.k_hbm = bf16[6,128,320]{2,1,0:T(8,128)(2,1)} copy(bf16[6,128,320]{1,2,0:T(8,128)(2,1)} %param.17) | data formatting | bytes 983040 | tf_op args[4]
  6.3 2.1 %copy.17.v_hbm = bf16[6,128,320]{2,1,0:T(8,128)(2,1)} copy(bf16[6,128,320]{1,2,0:T(8,128)(2,1)} %param.18) | data formatting | bytes 983040 | tf_op args[5]
  8.4 0.0 copy-done
  8.4 2.6 %copy.18.up_hbm = bf16[2880,360]{1,0:T(8,128)(2,1)} copy(bf16[2880,360]{0,1:T(8,128)(2,1)S(1)} %copy-done) | data formatting | bytes 4147200 | tf_op args[11]
  10.9 30.4 %shard_map.127 = bf16[6,2880]{1,0:T(8,128)(2,1)} custom-call(bf16[6,2880]{1,0:T(8,128)(2,1)} %q_ref.1, bf16[6,2880]{1,0:T(8,128)(2,1)} %res_ref.1, bf16[6,320]{1,0:T(8,128)(2,1)} %kn_ref.1, bf16[6,320]{1,0:T(8,128)(2,1)} %vn_ref.1, s32[6]{0:T(128)} %len_ref.1, f32[1,45]{1,0:T(1,128)} %bitcast.1, f32[1,2880]{1,0:T(1,128)} %reshape.7.gain_ref, ...), custom_call_target="tpu_custom_call" | custom-call | tf_op jit(solution)/shard_map/pallas_call | solution.py:425
  41.3 1.4 %copy.20 = bf16[6,2880]{1,0:T(8,128)(2,1)} copy(bf16[6,2880]{1,0:T(8,128)(2,1)} %shard_map.127) | data formatting | bytes 69120
Async XLA Ops:
  0.0 8.4 %copy-start = (bf16[2880,360]{0,1:T(8,128)(2,1)S(1)}, bf16[2880,360]{0,1:T(8,128)(2,1)}, u32[]{:S(2)}) copy-start(bf16[2880,360]{0,1:T(8,128)(2,1)} %param.24) | copy-start | bytes 6220804

commit v2 on v1

--- a/solution.py
+++ b/solution.py
@@ -17,6 +17,10 @@
 
 def iota(shape, dim):
     return lax.broadcasted_iota(jnp.int32, shape, dim)
+
+
+def dot_nt(a, b):
+    return lax.dot_general(a, b, (((1,), (1,)), ((), ())), preferred_element_type=F32)
 
 
 def spread_queries(q_ref, wide_ref, group_size):
@@ -42,7 +46,7 @@
 
 def attend(wide_ref, kn_ref, vn_ref, k_ref, v_ref, len_ref, sink_ref, ctx_ref, group_size):
     requests, head_rows, kv_width = wide_ref.shape
-    window = k_ref.shape[1]
+    window = k_ref.shape[2]
     heads = sink_ref.shape[1]
     scale = HD ** (-0.5)
     eye = iota((head_rows, heads), 0) == iota((head_rows, heads), 1)
@@ -58,10 +62,7 @@
         visible = (position >= 0) & (position >= length - window + 1)
         q = wide_ref[t]
         scores = (
-            lax.dot_general(
-                q.astype(BF16), k_ref[t], (((1,), (1,)), ((), ())), preferred_element_type=F32
-            )
-            * scale
+            jnp.dot(q.astype(BF16), k_ref[t], preferred_element_type=F32) * scale
         )
         scores = jnp.where(visible, scores, -1e30)
         fresh = (
@@ -75,7 +76,7 @@
         total = jnp.sum(weights, axis=1, keepdims=True) + fresh_weight + jnp.exp(sink - highest)
         probs = (weights / total).astype(BF16)
         fresh_prob = (fresh_weight / total).astype(BF16).astype(F32)
-        context = jnp.dot(probs, v_ref[t], preferred_element_type=F32)
+        context = dot_nt(probs, v_ref[t])
         context = context + fresh_prob * vn_ref[t : t + 1, :].astype(F32)
         context = jnp.where(own, context, 0.0)
         folded = jnp.zeros((head_rows, LANES), F32)
@@ -116,7 +117,9 @@
     hid_ref,
     norm_ref,
     rows_ref,
+    ids_wide,
     ids_pad,
+    logit_wide,
     logit_pad,
     packed_ref,
     recv_ref,
@@ -145,7 +148,6 @@
     heads = width // HD
     experts = n // 2
     group_size = heads // (kn_ref.shape[1] // HD)
-    depth = down_ref.shape[0]
 
     loads = [
         pltpu.make_async_copy(src, dst, load_sem.at[i])
@@ -156,7 +158,6 @@
     for load in loads:
         load.start()
 
-    recv_ref[...] = jnp.zeros_like(recv_ref)
     back_ref[...] = jnp.zeros_like(back_ref)
 
     barrier = pltpu.get_barrier_semaphore()
@@ -168,15 +169,21 @@
         pl.semaphore_signal(barrier, inc=1, device_id=(group, other, core), device_id_type=MESH)
 
     token_rows = 2 * SLOTS
-    ids_pad[...] = jnp.full(ids_pad.shape, -1, jnp.int32)
-    logit_pad[...] = jnp.zeros(logit_pad.shape, F32)
-    for side in range(2):
-        ids_pad[side * SLOTS : side * SLOTS + rows, :] = ids_ref[side * rows : (side + 1) * rows, :]
-        logit_pad[side * SLOTS : side * SLOTS + rows, :] = logit_ref[
-            side * rows : (side + 1) * rows, :
-        ]
-    ids = ids_pad[...]
-    logits = logit_pad[...]
+    picks = ids_ref.shape[0]
+
+    def by_token(src, wide, tall, fill):
+        wide[...] = jnp.full(wide.shape, fill, wide.dtype)
+        wide[:picks, : 2 * rows] = src[...]
+        turned = wide[...].T
+        tall[...] = jnp.full(tall.shape, fill, tall.dtype)
+        for side in range(2):
+            tall[side * SLOTS : side * SLOTS + rows, :] = turned[
+                side * rows : (side + 1) * rows, :
+            ]
+        return tall[:, :picks]
+
+    ids = by_token(ids_ref, ids_wide, ids_pad, -1)
+    logits = by_token(logit_ref, logit_wide, logit_pad, 0)
     gates = jnp.exp(logits - jnp.max(logits, axis=1, keepdims=True))
     gates = gates / jnp.sum(gates, axis=1, keepdims=True)
     earlier = (iota((token_rows, token_rows), 1) < iota((token_rows, token_rows), 0)).astype(F32)
@@ -212,10 +219,11 @@
         hid_ref[0:rows, columns] = both + res_ref[:, columns].astype(F32)
     hidden = hid_ref[...]
     inverse = lax.rsqrt(jnp.sum(hidden * hidden, axis=1, keepdims=True) / width + 1e-05)
-    norm_ref[0] = (hidden[:, :half] * inverse * gain_ref[:, :half]).astype(BF16)
+    gain = gain_ref[...].reshape(1, width)
+    norm_ref[0] = (hidden[:, :half] * inverse * gain[:, :half]).astype(BF16)
     norm_ref[1] = jnp.zeros(norm_ref.shape[1:], BF16)
     norm_ref[1, :, : width - half] = (
-        hidden[:, half:width] * inverse * gain_ref[:, half:]
+        hidden[:, half:width] * inverse * gain[:, half:]
     ).astype(BF16)
 
     pl.semaphore_wait(barrier, n)
@@ -318,9 +326,7 @@
         blocks = pl.ds(part * chunk, chunk)
         low = recv_ref[0, blocks].astype(F32).reshape(chunk_rows, half).astype(BF16)
         high = recv_ref[1, blocks].astype(F32).reshape(chunk_rows, half).astype(BF16)
-        value = jnp.dot(low, up_ref[:half, :], preferred_element_type=F32) + jnp.dot(
-            high[:, : width - half], up_ref[half:, :], preferred_element_type=F32
-        )
+        value = dot_nt(low, up_ref[:, :half]) + dot_nt(high[:, : width - half], up_ref[:, half:])
         value = value / (1.0 + jnp.exp(-value))
         act_ref[core, pl.ds(pl.multiple_of(part * chunk_rows, chunk_rows), chunk_rows), :] = (
             value.astype(BF16)
@@ -390,8 +396,8 @@
     theirs = mix_peer[...].astype(F32)
     low = jnp.where(core == 0, mine, theirs)
     high = jnp.where(core == 0, theirs, mine)
-    out_ref[:, :half] = (hid_ref[:, :half] + low)[:rows].astype(BF16)
-    out_ref[:, half:] = (hid_ref[:, half:width] + high[:, : width - half])[:rows].astype(BF16)
+    out_ref[:, :half] = (hid_ref[:, :half] + low)[:rows]
+    out_ref[:, half:] = (hid_ref[:, half:width] + high[:, : width - half])[:rows]
 
 
 def local(
@@ -424,21 +430,23 @@
     dma = pltpu.SemaphoreType.DMA
     return pl.pallas_call(
         functools.partial(kernel, n, capacity, half),
-        out_shape=jax.ShapeDtypeStruct((rows, width), BF16),
+        out_shape=jax.ShapeDtypeStruct((rows, width), F32),
         in_specs=[vmem] * 4 + [smem] + [vmem] * 4 + [anywhere] * 4,
         out_specs=vmem,
         scratch_shapes=[
-            pltpu.VMEM(key_cache.shape, BF16),
-            pltpu.VMEM(value_cache.shape, BF16),
-            pltpu.VMEM(up_weight.shape, BF16),
+            pltpu.VMEM((rows, key_cache.shape[2], key_cache.shape[1]), BF16),
+            pltpu.VMEM((rows, key_cache.shape[2], key_cache.shape[1]), BF16),
+            pltpu.VMEM((depth, width), BF16),
             pltpu.VMEM(down_weight.shape, BF16),
             pltpu.VMEM((rows, head_rows, key_new.shape[1]), F32),
             pltpu.VMEM((rows, head_rows, LANES), F32),
             pltpu.VMEM((SLOTS, 2 * half), F32),
             pltpu.VMEM((2, SLOTS, half), BF16),
             pltpu.VMEM((2, SLOTS, half), BF16),
-            pltpu.VMEM((2 * SLOTS, pick_count), jnp.int32),
-            pltpu.VMEM((2 * SLOTS, pick_count), F32),
+            pltpu.VMEM((8, LANES), jnp.int32),
+            pltpu.VMEM((2 * SLOTS, 8), jnp.int32),
+            pltpu.VMEM((8, LANES), F32),
+            pltpu.VMEM((2 * SLOTS, 8), F32),
             pltpu.VMEM((experts, SLOTS, half), BF16),
             pltpu.VMEM((2, n, SLOTS, half), BF16),
             pltpu.VMEM((2, n * SLOTS, depth), BF16),
@@ -468,14 +476,14 @@
         value_new,
         lengths,
         sink_logits.reshape(1, -1),
-        norm_gain.reshape(1, -1),
-        route_ids,
-        route_logits,
-        key_cache,
-        value_cache,
-        up_weight,
+        norm_gain,
+        route_ids.T,
+        route_logits.T,
+        jnp.swapaxes(key_cache, 1, 2),
+        jnp.swapaxes(value_cache, 1, 2),
+        up_weight.T,
         down_weight,
-    )
+    ).astype(BF16)
 
 
 def solution(mesh):

time: 43.1 us -> 32.6 us (0.76)
  local copies, waits for them, and re-layouts: 12.4 us -> 0 us
  other arithmetic: 0 us -> 1.52 us
    unnamed x8 -> x0, local copies, waits for them, and re-layouts: 11 us -> none
    convert_element_type x0 -> x1, other arithmetic: none -> 1.52 us  [local(): return pl.pallas_call(functools.partial(kernel, n, capacity, half), out_s...]
    reshape x1 -> x0, local copies, waits for them, and re-layouts: 1.31 us -> none  [local(): norm_gain.reshape(1, -1)]
    pallas_call x1, Pallas kernels: 30.4 us -> 30.8 us  [local(): pl.pallas_call(functools.partial(kernel, n, capacity, half), out_shape=ja...]
where the time goes in v2:
time: 32.6 us; the launch traced here: 32.4 us
  Pallas kernels  30.8 us (94%)
  other arithmetic  1.52 us (5%)
    pallas_call x1, Pallas kernels, local(): pl.pallas_call(functools.partial(kernel, n, capacity, half), out_shape=ja...  30.8 us
    convert_element_type x1, other arithmetic, local(): return pl.pallas_call(functools.partial(kernel, n, capacity, half), out_s...  1.52 us

profile of v2, /device:TPU:25, one launch (start us, length us, event | category | flops | bytes accessed | tf_op | source)
XLA Modules:
  0.0 32.4 jit_solution(2804448267859208920)
XLA Ops:
  0.0 30.8 %shard_map.127 = f32[6,2880]{1,0:T(8,128)} custom-call(bf16[6,2880]{1,0:T(8,128)(2,1)} %q_ref.1, bf16[6,2880]{1,0:T(8,128)(2,1)} %res_ref.1, bf16[6,320]{1,0:T(8,128)(2,1)} %kn_ref.1, bf16[6,320]{1,0:T(8,128)(2,1)} %vn_ref.1, s32[6]{0:T(128)} %len_ref.1, f32[1,45]{1,0:T(1,128)} %bitcast.11, f32[2880]{0:T(1024)} %gain_ref.1, s32[4,12]{1,0:T(4,128)} %bitcast.9, ...), custom_call_target="tpu_custom_call" | custom-call | tf_op jit(solution)/shard_map/pallas_call | solution.py:431
  30.8 1.5 %convert_element_type.3 = bf16[6,2880]{1,0:T(8,128)(2,1)} convert(f32[6,2880]{1,0:T(8,128)} %shard_map.127) | non-fusion elementwise | flops 17280 | bytes 103680 | tf_op jit(solution)/shard_map/convert_element_type | solution.py:486

commit v3 on v2

--- a/solution.py
+++ b/solution.py
@@ -94,6 +94,20 @@
     n,
     capacity,
     half,
+    q_hbm,
+    res_hbm,
+    kn_hbm,
+    vn_hbm,
+    len_hbm,
+    sink_hbm,
+    gain_hbm,
+    ids_hbm,
+    logit_hbm,
+    k_hbm,
+    v_hbm,
+    up_hbm,
+    down_hbm,
+    out_ref,
     q_ref,
     res_ref,
     kn_ref,
@@ -103,11 +117,6 @@
     gain_ref,
     ids_ref,
     logit_ref,
-    k_hbm,
-    v_hbm,
-    up_hbm,
-    down_hbm,
-    out_ref,
     k_ref,
     v_ref,
     up_ref,
@@ -149,24 +158,38 @@
     experts = n // 2
     group_size = heads // (kn_ref.shape[1] // HD)
 
+    barrier = pltpu.get_barrier_semaphore()
+    pl.semaphore_signal(barrier, inc=1, device_id=peer, device_id_type=MESH)
+
+    @pl.loop(1, n)
+    def _(step):
+        other = lax.rem(me + step, n)
+        pl.semaphore_signal(barrier, inc=1, device_id=(group, other, core), device_id_type=MESH)
+
     loads = [
         pltpu.make_async_copy(src, dst, load_sem.at[i])
         for i, (src, dst) in enumerate(
-            ((k_hbm, k_ref), (v_hbm, v_ref), (down_hbm, down_ref), (up_hbm, up_ref))
+            (
+                (ids_hbm, ids_ref),
+                (logit_hbm, logit_ref),
+                (q_hbm, q_ref),
+                (len_hbm, len_ref),
+                (k_hbm, k_ref),
+                (kn_hbm, kn_ref),
+                (sink_hbm, sink_ref),
+                (v_hbm, v_ref),
+                (vn_hbm, vn_ref),
+                (res_hbm, res_ref),
+                (gain_hbm, gain_ref),
+                (down_hbm, down_ref),
+                (up_hbm, up_ref),
+            )
         )
     ]
     for load in loads:
         load.start()
-
-    back_ref[...] = jnp.zeros_like(back_ref)
-
-    barrier = pltpu.get_barrier_semaphore()
-    pl.semaphore_signal(barrier, inc=1, device_id=peer, device_id_type=MESH)
-
-    @pl.loop(1, n)
-    def _(step):
-        other = lax.rem(me + step, n)
-        pl.semaphore_signal(barrier, inc=1, device_id=(group, other, core), device_id_type=MESH)
+    loads[0].wait()
+    loads[1].wait()
 
     token_rows = 2 * SLOTS
     picks = ids_ref.shape[0]
@@ -202,9 +225,16 @@
         chosen = jnp.where(place == slot.astype(F32), hot, 0.0)
         return chosen, gate * chosen
 
+    send_table, _ = tables(max(experts * SLOTS, LANES), SLOTS)
+    send_table = send_table.T[: experts * SLOTS].astype(BF16)
+    _, mixing = tables(n * SLOTS, 2 * SLOTS)
+    coarse = mixing.astype(BF16)
+    fine = (mixing - coarse.astype(F32)).astype(BF16)
+
+    loads[2].wait()
     spread_queries(q_ref, wide_ref, group_size)
-    loads[0].wait()
-    loads[1].wait()
+    for load in loads[3:11]:
+        load.wait()
     attend(wide_ref, kn_ref, vn_ref, k_ref, v_ref, len_ref, sink_ref, ctx_ref, group_size)
     hid_ref[...] = jnp.zeros_like(hid_ref)
     for tile in range((heads + 1) // 2):
@@ -242,13 +272,6 @@
     swap_rows.start()
     rows_ref[core] = norm_ref[core]
 
-    loads[2].wait()
-    down_half[0] = down_ref[:, :half]
-    down_half[1] = jnp.zeros(down_half.shape[1:], BF16)
-    down_half[1, :, : width - half] = down_ref[:, half:]
-
-    send_table, _ = tables(max(experts * SLOTS, LANES), SLOTS)
-    send_table = send_table.T[: experts * SLOTS].astype(BF16)
     swap_rows.wait()
     token_block = rows_ref[...].astype(F32).reshape(token_rows, half).astype(BF16)
     packed = jnp.dot(send_table, token_block, preferred_element_type=F32)
@@ -278,10 +301,17 @@
             device_id_type=MESH,
         )
 
-    @pl.loop(1, n)
-    def _(step):
-        go(step).start()
-
+    def far_first(turn):
+        return 1 + lax.rem(turn + n // 2 - 2, n - 1)
+
+    @pl.loop(1, n)
+    def _(turn):
+        go(far_first(turn)).start()
+
+    loads[11].wait()
+    down_half[0] = down_ref[:, :half]
+    down_half[1] = jnp.zeros(down_half.shape[1:], BF16)
+    down_half[1, :, : width - half] = down_ref[:, half:]
     swap_down = to_peer(down_half.at[1 - core], down_peer, 1)
     swap_down.start()
 
@@ -299,7 +329,8 @@
     forward(packed_ref.at[me // 2, used], me).start()
 
     @pl.loop(1, n)
-    def _(step):
+    def _(turn):
+        step = far_first(n - turn)
         source = lax.rem(me + n - step, n)
         block = recv_ref.at[core, source, used]
         come(step, block, go_send, go_recv)[1].wait_recv()
@@ -317,7 +348,7 @@
             device_id_type=MESH,
         ).wait_recv()
 
-    loads[3].wait()
+    loads[12].wait()
     chunk = min(n, 16)
     chunk_rows = chunk * SLOTS
 
@@ -358,13 +389,10 @@
         )
 
     @pl.loop(1, n)
-    def _(step):
-        give_back(step).start()
+    def _(turn):
+        give_back(far_first(turn)).start()
 
     back_ref[me] = sent_ref[me]
-    _, mixing = tables(n * SLOTS, 2 * SLOTS)
-    coarse = mixing.astype(BF16)
-    fine = (mixing - coarse.astype(F32)).astype(BF16)
 
     @pl.loop(1, n)
     def _(step):
@@ -379,7 +407,9 @@
         source = lax.rem(me + n - step, n)
         come(step, back_ref.at[source, used], ret_send, ret_recv)[1].wait_recv()
 
-    returned = back_ref[...].astype(F32).reshape(n * SLOTS, half).astype(BF16)
+    returned = back_ref[...].astype(F32)
+    returned = jnp.where(iota(returned.shape, 1) < capacity, returned, 0.0)
+    returned = returned.reshape(n * SLOTS, half).astype(BF16)
     mixed = jnp.dot(coarse, returned, preferred_element_type=F32) + jnp.dot(
         fine, returned, preferred_element_type=F32
     )
@@ -425,15 +455,23 @@
     head_rows = -(-heads // 8) * 8
     depth = up_weight.shape[1]
     vmem = pl.BlockSpec(memory_space=pltpu.VMEM)
-    smem = pl.BlockSpec(memory_space=pltpu.SMEM)
     anywhere = pl.BlockSpec(memory_space=pl.ANY)
     dma = pltpu.SemaphoreType.DMA
     return pl.pallas_call(
         functools.partial(kernel, n, capacity, half),
         out_shape=jax.ShapeDtypeStruct((rows, width), F32),
-        in_specs=[vmem] * 4 + [smem] + [vmem] * 4 + [anywhere] * 4,
+        in_specs=[anywhere] * 13,
         out_specs=vmem,
         scratch_shapes=[
+            pltpu.VMEM(queries.shape, BF16),
+            pltpu.VMEM(residual.shape, BF16),
+            pltpu.VMEM(key_new.shape, BF16),
+            pltpu.VMEM(value_new.shape, BF16),
+            pltpu.SMEM(lengths.shape, jnp.int32),
+            pltpu.VMEM((1, heads), F32),
+            pltpu.VMEM(norm_gain.shape, F32),
+            pltpu.VMEM(route_ids.shape[::-1], jnp.int32),
+            pltpu.VMEM(route_ids.shape[::-1], F32),
             pltpu.VMEM((rows, key_cache.shape[2], key_cache.shape[1]), BF16),
             pltpu.VMEM((rows, key_cache.shape[2], key_cache.shape[1]), BF16),
             pltpu.VMEM((depth, width), BF16),
@@ -456,7 +494,7 @@
             pltpu.VMEM((n, SLOTS, half), BF16),
             pltpu.VMEM((2, SLOTS, half), BF16),
             pltpu.VMEM((SLOTS, half), BF16),
-            dma((4,)),
+            dma((13,)),
             dma((4,)),
             dma((4,)),
             dma((n,)),

time: 32.6 us -> 34.9 us (1.071)
  the two profiles are of different devices: /device:TPU:25 before, /device:TPU:0 now
where the time goes in v3:
time: 34.9 us; the launch traced here: 34.7 us
  Pallas kernels  33.2 us (95%)
  other arithmetic  1.52 us (4%)
    pallas_call x1, Pallas kernels, local(): pl.pallas_call(functools.partial(kernel, n, capacity, half), out_shape=ja...  33.2 us
    convert_element_type x1, other arithmetic, local(): return pl.pallas_call(functools.partial(kernel, n, capacity, half), out_s...  1.52 us

profile of v3, /device:TPU:0, one launch (start us, length us, event | category | flops | bytes accessed | tf_op | source)
XLA Modules:
  0.0 34.7 jit_solution(1825565561438267026)
XLA Ops:
  0.0 33.2 %shard_map.127 = f32[6,2880]{1,0:T(8,128)} custom-call(bf16[6,2880]{1,0:T(8,128)(2,1)} %q_hbm.1, bf16[6,2880]{1,0:T(8,128)(2,1)} %res_hbm.1, bf16[6,320]{1,0:T(8,128)(2,1)} %kn_hbm.1, bf16[6,320]{1,0:T(8,128)(2,1)} %vn_hbm.1, s32[6]{0:T(128)} %len_hbm.1, f32[1,45]{1,0:T(1,128)} %bitcast.11, f32[2880]{0:T(1024)} %gain_hbm.1, s32[4,12]{1,0:T(4,128)} %bitcast.9, ...), custom_call_target="tpu_custom_call" | custom-call | tf_op jit(solution)/shard_map/pallas_call | solution.py:460
  33.2 1.5 %convert_element_type.3 = bf16[6,2880]{1,0:T(8,128)(2,1)} convert(f32[6,2880]{1,0:T(8,128)} %shard_map.127) | non-fusion elementwise | flops 17280 | bytes 103680 | tf_op jit(solution)/shard_map/convert_element_type | solution.py:524

commit v4 on v3

--- a/solution.py
+++ b/solution.py
@@ -301,12 +301,9 @@
             device_id_type=MESH,
         )
 
-    def far_first(turn):
-        return 1 + lax.rem(turn + n // 2 - 2, n - 1)
-
-    @pl.loop(1, n)
-    def _(turn):
-        go(far_first(turn)).start()
+    @pl.loop(1, n)
+    def _(step):
+        go(step).start()
 
     loads[11].wait()
     down_half[0] = down_ref[:, :half]
@@ -329,8 +326,7 @@
     forward(packed_ref.at[me // 2, used], me).start()
 
     @pl.loop(1, n)
-    def _(turn):
-        step = far_first(n - turn)
+    def _(step):
         source = lax.rem(me + n - step, n)
         block = recv_ref.at[core, source, used]
         come(step, block, go_send, go_recv)[1].wait_recv()
@@ -389,8 +385,8 @@
         )
 
     @pl.loop(1, n)
-    def _(turn):
-        give_back(far_first(turn)).start()
+    def _(step):
+        give_back(step).start()
 
     back_ref[me] = sent_ref[me]
 

time: 34.9 us -> 32 us (0.917)
  the two profiles are of different devices: /device:TPU:0 before, /device:TPU:25 now
where the time goes in v4:
time: 32 us; the launch traced here: 31.8 us
  Pallas kernels  30.3 us (95%)
  other arithmetic  1.52 us (5%)
    pallas_call x1, Pallas kernels, local(): pl.pallas_call(functools.partial(kernel, n, capacity, half), out_shape=ja...  30.3 us
    convert_element_type x1, other arithmetic, local(): return pl.pallas_call(functools.partial(kernel, n, capacity, half), out_s...  1.52 us

profile of v4, /device:TPU:25, one launch (start us, length us, event | category | flops | bytes accessed | tf_op | source)
XLA Modules:
  0.0 31.8 jit_solution(17866930520995583792)
XLA Ops:
  0.0 30.3 %shard_map.127 = f32[6,2880]{1,0:T(8,128)} custom-call(bf16[6,2880]{1,0:T(8,128)(2,1)} %q_hbm.1, bf16[6,2880]{1,0:T(8,128)(2,1)} %res_hbm.1, bf16[6,320]{1,0:T(8,128)(2,1)} %kn_hbm.1, bf16[6,320]{1,0:T(8,128)(2,1)} %vn_hbm.1, s32[6]{0:T(128)} %len_hbm.1, f32[1,45]{1,0:T(1,128)} %bitcast.11, f32[2880]{0:T(1024)} %gain_hbm.1, s32[4,12]{1,0:T(4,128)} %bitcast.9, ...), custom_call_target="tpu_custom_call" | custom-call | tf_op jit(solution)/shard_map/pallas_call | solution.py:456
  30.3 1.5 %convert_element_type.3 = bf16[6,2880]{1,0:T(8,128)(2,1)} convert(f32[6,2880]{1,0:T(8,128)} %shard_map.127) | non-fusion elementwise | flops 17280 | bytes 103680 | tf_op jit(solution)/shard_map/convert_element_type | solution.py:520
